TPU v7x, 32 devices: a whole 2x2x4 slice. The times are simulated.
32 devices in a mesh: section: 2 (over x), lat: 4 (over z), lon: 4 (over y, core).
Axes of the slice: x: 2, y: 2, z: 4, core: 2. Of those that a mesh axis runs over, the one named last changes fastest.
Arguments:
- state: bfloat16 [2, 112, 360, 1024], P('section', 'lat', 'lon'), may hold values from -6 to 6
- fresh: bfloat16 [112, 360, 1024], P('lat', 'lon'), may hold values from -6 to 6
- cutoff: int32 [3], replicated, may hold values from 0 to 15
- plan: int32 [2, 2], replicated, may hold values from 0 to 1
- lmax: int32 [2], replicated, may hold values from 56 to 112, as said below
- mmax: int32 [2], replicated, may hold values from 24 to 96, as said below
- cutoff_table: float32 [16, 1024], replicated, may hold values from -3 to 3
- norm_gains: float32 [2, 2, 2, 1024], P('section'), may hold values from 0.1 to 1.9
- filters: float32 [2, 2, 2, 112, 1024], P('section', None, None, None, 'lon'), may hold values from -5 to 5
- w_in: bfloat16 [2, 2, 1024, 4096], P('section', None, 'lat'), may hold values from -0.1875 to 0.1875
- w_out: bfloat16 [2, 2, 1024, 4096], P('section', None, 'lat'), may hold values from -0.09375 to 0.09375
Outputs:
- first_pass: bfloat16 [2, 112, 360, 1024], P('section', 'lat', 'lon')
- second_pass: bfloat16 [2, 112, 360, 1024], P('section', 'lat', 'lon')
Inputs may be any that keep to these rules, and one draw needn't show every extreme that they name: `lmax`: some section keeps all 112 degrees in every draw. `mmax`: some section keeps all 96 wavenumbers in every draw.
All inputs are finite; a program needn't handle non-finite values.
Results may differ from a plain program's by a relative error of at most 0.01.
Values may be sent and summed in bfloat16 or wider, within the bound.
No kernel may reach another device: no remote copies, remote signals or barrier semaphores. Data moves between devices by JAX's collectives and lax.ppermute only.
A program may use at most 384 MiB of HBM per device.

v0:
```python
import math

import jax
import jax.numpy as jnp
from jax import lax
from jax.sharding import PartitionSpec as P

MM = 96


def passed_along(value, axis, steps):
    count = lax.axis_size(axis)
    leading, last = (max(0, -steps), min(count, count - steps))
    return lax.ppermute(value, axis, [(source, source + steps) for source in range(leading, last)])


def legendre_table(orders, n_rows, n_degrees):
    rows = jnp.arange(n_rows, dtype=jnp.float32)
    theta = math.pi * (rows + 0.5) / n_rows
    cosine = jnp.cos(theta)
    sine = jnp.sin(theta)
    order = orders[:, None]
    log_start = (
        0.5 * jnp.log((2.0 * order + 1.0) / (4.0 * math.pi))
        + jax.scipy.special.gammaln(order + 0.5)
        - jax.scipy.special.gammaln(0.5)
        - jax.scipy.special.gammaln(order + 1.0)
        + order * jnp.log(sine)[None, :]
    )
    start = jnp.exp(log_start)

    def advance(carry, degree):
        last, before = carry
        level = degree.astype(jnp.float32)
        coef_a = jnp.sqrt(
            jnp.maximum(4.0 * level * level - 1.0, 1.0)
            / jnp.maximum(level * level - order * order, 1.0)
        )
        coef_b = jnp.sqrt(
            jnp.maximum((level - 1.0) ** 2 - order * order, 0.0)
            / jnp.maximum(4.0 * (level - 1.0) ** 2 - 1.0, 1.0)
        )
        general = coef_a * (cosine[None, :] * last - coef_b * before)
        fresh_row = jnp.where(
            level < order, jnp.zeros_like(start), jnp.where(level == order, start, general)
        )
        return ((fresh_row, last), fresh_row)

    _, table = lax.scan(
        advance,
        (jnp.zeros_like(start), jnp.zeros_like(start)),
        jnp.arange(n_degrees, dtype=jnp.int32),
    )
    quad = 2.0 * math.pi * (math.pi / n_rows) * sine
    return (table, table * quad[None, None, :])


def fourier_tables(n_lon):
    columns = jnp.arange(n_lon, dtype=jnp.int32)
    orders = jnp.arange(MM, dtype=jnp.int32)
    phase = 2.0 * math.pi * (columns[:, None] * orders[None, :] % n_lon).astype(jnp.float32) / n_lon
    cos_fwd = jnp.cos(phase) / n_lon
    sin_fwd = -jnp.sin(phase) / n_lon
    weight = jnp.where(orders == 0, 1.0, 2.0).astype(jnp.float32)[:, None]
    inverse = jnp.stack([weight * jnp.cos(phase).T, -weight * jnp.sin(phase).T], 0)
    return (cos_fwd, sin_fwd, inverse)


def layer_norm(values, gain):
    center = values - jnp.mean(values, axis=-1, keepdims=True)
    spread = jnp.mean(center * center, axis=-1, keepdims=True)
    return center * lax.rsqrt(spread + 1e-05) * gain


def pick(stack, index):
    return lax.dynamic_index_in_dim(stack, index, 0, keepdims=False)


def local(state, fresh, cutoff, plan, lmax, mmax, cutoff_table, norm_gains, filters, w_in, w_out):
    highest = lax.Precision.HIGHEST
    section_idx = lax.axis_index("section")
    lat_idx = lax.axis_index("lat")
    n_section = lax.axis_size("section")
    n_lat = lax.axis_size("lat")
    n_lon = lax.axis_size("lon")
    n_rows, n_cols, width = fresh.shape
    n_degrees = filters.shape[3]
    all_rows = n_rows * n_lat
    all_cols = n_cols * n_lon
    m_local = MM // n_lat
    m_global = lat_idx * m_local + jnp.arange(m_local, dtype=jnp.int32)
    plain, weighted = legendre_table(m_global.astype(jnp.float32), all_rows, n_degrees)
    cos_fwd, sin_fwd, inverse = fourier_tables(all_cols)
    l_max = pick(lmax, section_idx)
    m_max = pick(mmax, section_idx)
    keep = (
        (jnp.arange(n_degrees, dtype=jnp.int32) < l_max)[:, None] & (m_global < m_max)[None, :]
    ).astype(jnp.float32)[:, :, None]

    def run_block(tokens, tick):
        block_idx = pick(plan[tick], section_idx)
        cut = pick(cutoff, tick - section_idx + n_section - 1)
        gains = pick(norm_gains[0], block_idx)
        filt = pick(filters[0], block_idx)
        weight_in = pick(w_in[0], block_idx)
        weight_out = pick(w_out[0], block_idx)
        onehot = (jnp.arange(cutoff_table.shape[0], dtype=jnp.int32) == cut).astype(jnp.float32)
        embed = jnp.dot(onehot, cutoff_table, precision=highest)
        base = tokens.astype(jnp.float32) + embed
        normed = layer_norm(base, gains[0]).astype(jnp.bfloat16)
        by_lon = lax.all_to_all(normed, "lon", split_axis=2, concat_axis=1, tiled=True)
        wide = by_lon.astype(jnp.float32)
        real_part = jnp.einsum("jkc,km->jmc", wide, cos_fwd, precision=highest)
        imag_part = jnp.einsum("jkc,km->jmc", wide, sin_fwd, precision=highest)
        spectrum = jnp.stack([real_part, imag_part], 1).astype(jnp.bfloat16)
        by_mode = lax.all_to_all(spectrum, "lat", split_axis=2, concat_axis=0, tiled=True)
        coeff = jnp.einsum(
            "lmj,jrmc->rlmc", weighted, by_mode.astype(jnp.float32), precision=highest
        )
        filt_re = filt[0][:, None, :]
        filt_im = filt[1][:, None, :]
        out_re = keep * (coeff[0] * filt_re - coeff[1] * filt_im)
        out_im = keep * (coeff[0] * filt_im + coeff[1] * filt_re)
        synthesis = jnp.einsum(
            "lmj,rlmc->jrmc", plain, jnp.stack([out_re, out_im], 0), precision=highest
        ).astype(jnp.bfloat16)
        by_row = lax.all_to_all(synthesis, "lat", split_axis=0, concat_axis=2, tiled=True)
        spectral = jnp.einsum(
            "jrmc,rmk->jkc", by_row.astype(jnp.float32), inverse, precision=highest
        ).astype(jnp.bfloat16)
        spectral = lax.all_to_all(spectral, "lon", split_axis=1, concat_axis=2, tiled=True)
        mixed = base + spectral.astype(jnp.float32)
        normed_two = layer_norm(mixed, gains[1]).astype(jnp.bfloat16)
        flat = normed_two.reshape(n_rows * n_cols, width)
        before_act = jnp.dot(
            flat,
            lax.all_gather(weight_in, "lat", axis=0, tiled=True),
            preferred_element_type=jnp.float32,
        )
        hidden = jax.nn.gelu(before_act).astype(jnp.bfloat16)
        projected = lax.dot_general(
            hidden,
            lax.all_gather(weight_out, "lat", axis=0, tiled=True),
            (((1,), (1,)), ((), ())),
            preferred_element_type=jnp.float32,
        )
        result = mixed + projected.reshape(mixed.shape)
        return result.astype(jnp.bfloat16)

    first_out = run_block(state[0], 0)
    handed = passed_along(first_out, "section", 1)
    entering = jnp.where(section_idx == 0, fresh, handed)
    second_out = run_block(entering, 1)
    return (first_out[None], second_out[None])


def solution(mesh):
    return jax.shard_map(
        local,
        mesh=mesh,
        in_specs=(
            P("section", "lat", "lon", None),
            P("lat", "lon", None),
            P(),
            P(),
            P(),
            P(),
            P(),
            P("section", None, None, None),
            P("section", None, None, None, "lon"),
            P("section", None, "lat", None),
            P("section", None, "lat", None),
        ),
        out_specs=(P("section", "lat", "lon", None), P("section", "lat", "lon", None)),
        check_vma=False,
    )
```

profile of v0, /device:TPU:0, one launch (start us, length us, event | category | flops | bytes accessed | tf_op | source)
XLA Modules:
  0.0 1451.1 jit_solution(14158678115372856451)
XLA Ops:
  21.4 7.0 multiply_convert_fusion.2
  28.4 12.0 copy.147
  40.4 5.6 all-to-all-start
  51.5 88.3 %all-to-all-done = bf16[28,90,1024]{1,0,2:T(8,128)(2,1)} async-done(((bf16[28,90,1024]{1,0,2:T(8,128)(2,1)}), bf16[28,90,1024]{1,0,2:T(8,128)(2,1)}, u32[]{:S(2)}, u32[]{:S(2)}) %all-to-all-start) | async-done | bytes 5160992 | tf_op jit(solution)/shard_map/all_to_all | solution.py:111
  139.9 14.5 copy.148
  154.3 8.3 all_to_all.95
  162.6 6.3 fusion.72
  177.4 6.0 all-to-all-start.1
  183.4 162.5 %while.20 = (s32[]{:T(128)}, f32[24,112]{1,0:T(8,128)S(1)}, f32[24,112]{1,0:T(8,128)S(1)}, f32[112,24,112]{2,1,0:T(8,128)S(1)}, s32[112]{0:T(128)S(1)}, /*index=...) while((s32[]{:T(128)}, f32[24,112]{1,0:T(8,128)S(1)}, ...), condition=%wide.region_3.4_spmd.clone.clone.clone, body=%wide.region_2.3_spmd.clone.clone.clone.sunk | while | flops 24742 | bytes 66539 | solution.py:49
  379.5 128.0 %all-to-all-done.2 = bf16[112,2,24,256]{3,1,2,0:T(2,128)(2,1)S(1)} async-done(((bf16[112,2,24,256]{3,1,2,0:T(2,128)(2,1)}), bf16[112,2,24,256]{3,1,2,0:T(2,128)(2,1)S(1)}, u32[]{:S(2)}, u32[]{:S(2)}) %all-to-all-start.2) | async-done | bytes 2752544 | tf_op jit(solution)/shard_map/all_to_all | solution.py:127
  522.2 8.2 reshape.641
  530.4 58.2 %all-to-all-done.3 = bf16[28,360,256]{2,0,1:T(8,128)(2,1)} async-done(((bf16[28,360,256]{2,0,1:T(8,128)(2,1)}), bf16[28,360,256]{2,0,1:T(8,128)(2,1)}, u32[]{:S(2)}, u32[]{:S(2)}) %all-to-all-start.3) | async-done | bytes 5160992 | tf_op jit(solution)/shard_map/all_to_all | solution.py:131
  588.6 9.5 copy_convert_fusion.1
  598.1 11.6 reshape.645
  609.7 14.5 copy.160
  624.2 14.0 reshape.643
  638.1 7.3 fusion.57
  645.5 8.0 multiply_reduce_fusion.2
  653.7 10.4 copy.191
  664.1 38.2 %fusion.16.clone.4 = bf16[2520,4096]{1,0:T(8,128)(2,1)} fusion(bf16[1,1,1024,4096]{3,2,1,0:T(8,128)(2,1)} %all-gather.9.cloned.1.call-done, f32[2520,1024]{1,0:T(8,128)} %bitcast.198, f32[2520,1024]{1,0:T(8,128)} %reshape.641, f32[1024]{0:T(1024)S(1)} %bitcast.218, f32[2520]{0:T(1024)S(1)} %rsqrt.37, f32[2520]{0:T(1024)S(1)} %div.110, ...), kind=kOutput, calls=%fused_computation.24.clone.clone.clone.1 | convolution fusion | flops 21247672320 | bytes 49704640 | tf_op jit(solution)/shard_map/dot_general | solution.py:135
  702.3 28.7 %fusion.34 = f32[2520,1024]{1,0:T(8,128)} fusion(bf16[1,1,1024,4096]{3,2,1,0:T(8,128)(2,1)} %all-gather.11.cloned.1.call-done, bf16[2520,4096]{1,0:T(8,128)(2,1)} %fusion.16.clone.4), kind=kOutput, calls=%fused_computation.56 | convolution fusion | flops 21139292160 | bytes 39354368 | tf_op jit(solution)/shard_map/dot_general | solution.py:141
  730.9 11.1 reshape.636
  742.0 12.8 add_convert_fusion.1
  754.8 5.8 collective-permute-start
  761.3 114.8 %collective-permute-done = bf16[28,90,1024]{2,1,0:T(8,128)(2,1)} collective-permute-done((bf16[28,90,1024]{2,1,0:T(8,128)(2,1)}, bf16[28,90,1024]{2,1,0:T(8,128)(2,1)}, u32[]{:S(2)}, u32[]{:S(2)}) %collective-permute-start) | collective-permute-done | bytes 5160992 | tf_op jit(solution)/shard_map/ppermute | solution.py:14
  887.1 12.0 copy.163
  905.5 92.4 %all-to-all-done.4 = bf16[28,90,1024]{1,0,2:T(8,128)(2,1)} async-done(((bf16[28,90,1024]{1,0,2:T(8,128)(2,1)}), bf16[28,90,1024]{1,0,2:T(8,128)(2,1)}, u32[]{:S(2)}, u32[]{:S(2)}) %all-to-all-start.4) | async-done | bytes 5160992 | tf_op jit(solution)/shard_map/all_to_all | solution.py:111
  997.9 14.9 %copy.164 = bf16[28,90,4,256]{3,1,2,0:T(8,128)(2,1)} copy(bf16[28,90,4,256]{1,0,3,2:T(8,128)(2,1)} %bitcast.41) | data formatting | bytes 10321920 | tf_op jit(solution)/shard_map/all_to_all | solution.py:111
  1012.7 8.3 all_to_all.108
  1021.0 6.3 fusion.74
  1034.3 80.7 %all_to_all.126 = bf16[28,2,96,256]{3,1,0,2:T(2,128)(2,1)S(1)} all-to-all(bf16[28,2,96,256]{3,1,0,2:T(2,128)(2,1)S(1)} %copy.165), channel_id=1, replica_groups=mesh['section'=2,'lat'=4,'lon'=4] {'lat'}, dimensions={2} | all-to-all | bytes 5505024 | tf_op jit(solution)/shard_map/all_to_all | solution.py:116
  1128.8 64.8 %all_to_all.127 = bf16[112,2,24,256]{3,1,2,0:T(2,128)(2,1)S(1)} all-to-all(bf16[112,2,24,256]{3,1,2,0:T(2,128)(2,1)S(1)} %copy.171), channel_id=1, replica_groups=mesh['section'=2,'lat'=4,'lon'=4] {'lat'}, dimensions={0} | all-to-all | bytes 5505024 | tf_op jit(solution)/shard_map/all_to_all | solution.py:127
  1209.0 10.9 reshape.635
  1219.9 13.8 reshape.640
  1233.7 12.9 add_convert_fusion.2
  1246.6 28.2 %all-to-all-done.7 = bf16[28,360,256]{2,0,1:T(8,128)(2,1)} async-done(((bf16[28,360,256]{2,0,1:T(8,128)(2,1)}), bf16[28,360,256]{2,0,1:T(8,128)(2,1)}, u32[]{:S(2)}, u32[]{:S(2)}) %all-to-all-start.7) | async-done | bytes 5160992 | tf_op jit(solution)/shard_map/all_to_all | solution.py:131
  1274.8 9.6 copy_convert_fusion
  1284.5 11.7 reshape.648
  1296.2 14.5 %copy.176 = f32[28,90,4,256]{3,2,1,0:T(4,128)} copy(f32[28,90,4,256]{3,1,2,0:T(8,128)} %bitcast.187) | data formatting | bytes 20643840 | tf_op jit(solution)/shard_map/convert_element_type | solution.py:132
  1310.7 14.0 reshape.644
  1324.7 7.4 fusion.157
  1332.1 8.1 multiply_reduce_fusion
  1340.3 8.4 multiply_convert_fusion
  1348.7 7.9 reshape.637
  1356.6 35.3 %fusion.24.clone.4 = bf16[2520,4096]{1,0:T(8,128)(2,1)} fusion(bf16[2520,1024]{1,0:T(8,128)(2,1)} %reshape.637, bf16[1,1,1024,4096]{3,2,1,0:T(8,128)(2,1)} %all-gather.13.cloned.1.call-done), kind=kOutput, calls=%fused_computation.32.clone.clone.clone.1 | convolution fusion | flops 21232189440 | bytes 34193408 | tf_op jit(solution)/shard_map/dot_general | solution.py:135
  1391.9 28.8 %fusion.30 = f32[2520,1024]{1,0:T(8,128)} fusion(bf16[1,1,1024,4096]{3,2,1,0:T(8,128)(2,1)} %all-gather.15.cloned.1.call-done, bf16[2520,4096]{1,0:T(8,128)(2,1)} %fusion.24.clone.4), kind=kOutput, calls=%fused_computation.53 | convolution fusion | flops 21139292160 | bytes 39354368 | tf_op jit(solution)/shard_map/dot_general | solution.py:141
  1420.7 10.8 reshape.638
  1431.5 12.8 fusion.38
  (700 shorter events, 210.5 us)
Async XLA Ops:
  7.2 5.5 copy-start
  11.1 6.3 copy-start.2
  13.6 7.2 copy-start.22
  40.4 99.5 %all-to-all-start = ((bf16[28,90,1024]{1,0,2:T(8,128)(2,1)}), bf16[28,90,1024]{1,0,2:T(8,128)(2,1)}, u32[]{:S(2)}, u32[]{:S(2)}) async-start(bf16[28,90,1024]{1,0,2:T(8,128)(2,1)} %copy.147), calls=%async_computation | async-start | bytes 16777216 | tf_op jit(solution)/shard_map/all_to_all | solution.py:111
  46.0 618.0 %all-gather.9.cloned.1.call-start = ((), (), s32[]{:S(2)}) async-start(), calls=%async_computation.8 | async-start | bytes 10485760 | tf_op jit(solution)/shard_map/all_gather | solution.py:137
  162.6 6.3 copy-start.4
  173.0 172.9 %copy-start.23 = (s32[2]{0:T(128)S(1)}, s32[2]{0:T(128)}, u32[]{:S(2)}) copy-start(s32[2]{0:T(128)} %param.18) | copy-start | bytes 28
  173.1 173.5 %copy-start.24 = (s32[2]{0:T(128)S(1)}, s32[2]{0:T(128)}, u32[]{:S(2)}) copy-start(s32[2]{0:T(128)} %param.17) | copy-start | bytes 28
  177.4 171.6 %copy-start.17 = (f32[1,2,2,112,256]{4,3,2,1,0:T(8,128)S(1)}, f32[1,2,2,112,256]{4,3,2,1,0:T(8,128)}, u32[]{:S(2)}) copy-start(f32[1,2,2,112,256]{4,3,2,1,0:T(8,128)} %param.21) | copy-start | bytes 1376260
  177.4 173.9 %all-to-all-start.1 = ((bf16[28,2,96,256]{3,1,0,2:T(2,128)(2,1)}), bf16[28,2,96,256]{3,1,0,2:T(2,128)(2,1)}, u32[]{:S(2)}, u32[]{:S(2)}) async-start(bf16[28,2,96,256]{3,1,0,2:T(2,128)(2,1)} %copy.149), calls=%async_computation.1 | async-start | bytes 5505024 | tf_op jit(solution)/shard_map/all_to_all | solution.py:116
  345.9 3.9 copy-start.10
  347.7 11.6 copy-start.6
  349.9 8.5 copy-start.18
  351.3 3.2 copy-start.8
  368.2 139.3 %all-to-all-start.2 = ((bf16[112,2,24,256]{3,1,2,0:T(2,128)(2,1)}), bf16[112,2,24,256]{3,1,2,0:T(2,128)(2,1)S(1)}, u32[]{:S(2)}, u32[]{:S(2)}) async-start(bf16[112,2,24,256]{3,1,2,0:T(2,128)(2,1)} %copy.155), calls=%async_computation.2 | async-start | bytes 5505024 | tf_op jit(solution)/shard_map/all_to_all | solution.py:127
  373.3 329.0 %all-gather.11.cloned.1.call-start = ((), (), s32[]{:S(2)}) async-start(), calls=%async_computation.9 | async-start | bytes 10485760 | tf_op jit(solution)/shard_map/all_gather | solution.py:143
  378.9 129.4 %copy-start.11 = (f32[1,96,360]{2,1,0:T(8,128)}, f32[1,96,360]{2,1,0:T(8,128)S(1)}, u32[]{:S(2)}) copy-start(f32[1,96,360]{2,1,0:T(8,128)S(1)} %cosine_multiply_fusion.1) | copy-start | bytes 414724
  379.5 128.8 %copy-start.13 = (f32[1,96,360]{2,1,0:T(8,128)}, f32[1,96,360]{2,1,0:T(8,128)S(1)}, u32[]{:S(2)}) copy-start(f32[1,96,360]{2,1,0:T(8,128)S(1)} %sine_multiply_fusion) | copy-start | bytes 414724
  516.7 71.8 %all-to-all-start.3 = ((bf16[28,360,256]{2,0,1:T(8,128)(2,1)}), bf16[28,360,256]{2,0,1:T(8,128)(2,1)}, u32[]{:S(2)}, u32[]{:S(2)}) async-start(bf16[28,360,256]{2,0,1:T(8,128)(2,1)} %copy.158), calls=%async_computation.3 | async-start | bytes 11796480 | tf_op jit(solution)/shard_map/all_to_all | solution.py:131
  754.8 121.3 %collective-permute-start = (bf16[28,90,1024]{2,1,0:T(8,128)(2,1)}, bf16[28,90,1024]{2,1,0:T(8,128)(2,1)}, u32[]{:S(2)}, u32[]{:S(2)}) collective-permute-start(bf16[28,90,1024]{2,1,0:T(8,128)(2,1)} %add_convert_fusion.1), channel_id=1, source_target_pairs={{0,16},{1,17},{2,18},{3,19},{4,20},{5,21},{6,22},{7,23},{8,24},{9,... | collective-permute-start | bytes 15482888 | tf_op jit(solution)/shard_map/ppermute | solution.py:14
  880.7 2.5 copy-start.3
  880.7 2.4 copy-start.21
  899.1 98.8 %all-to-all-start.4 = ((bf16[28,90,1024]{1,0,2:T(8,128)(2,1)}), bf16[28,90,1024]{1,0,2:T(8,128)(2,1)}, u32[]{:S(2)}, u32[]{:S(2)}) async-start(bf16[28,90,1024]{1,0,2:T(8,128)(2,1)} %copy.163), calls=%async_computation.4 | async-start | bytes 16777216 | tf_op jit(solution)/shard_map/all_to_all | solution.py:111
  904.7 451.9 %all-gather.13.cloned.1.call-start = ((), (), s32[]{:S(2)}) async-start(), calls=%async_computation.10 | async-start | bytes 10485760 | tf_op jit(solution)/shard_map/all_gather | solution.py:137
  1021.0 6.3 copy-start.5
  1115.0 1.3 copy-start.9
  1115.9 4.3 copy-start.15
  1115.9 4.3 copy-start.16
  1115.9 4.3 copy-start.19
  1120.2 1.3 copy-start.7
  1193.7 0.9 copy-start.12
  1193.7 1.0 copy-start.14
  1203.1 71.7 %all-to-all-start.7 = ((bf16[28,360,256]{2,0,1:T(8,128)(2,1)}), bf16[28,360,256]{2,0,1:T(8,128)(2,1)}, u32[]{:S(2)}, u32[]{:S(2)}) async-start(bf16[28,360,256]{2,0,1:T(8,128)(2,1)} %copy.174), calls=%async_computation.7 | async-start | bytes 11796480 | tf_op jit(solution)/shard_map/all_to_all | solution.py:131
  1208.4 183.5 %all-gather.15.cloned.1.call-start = ((), (), s32[]{:S(2)}) async-start(), calls=%async_computation.11 | async-start | bytes 10485760 | tf_op jit(solution)/shard_map/all_gather | solution.py:143
  1324.7 15.6 %slice-start = ((s8[5505024]{0:T(1024)(128)(4,1)}), s8[4194304]{0:T(1024)(128)(4,1)S(1)}, s32[]{:S(2)}) async-start(s8[5505024]{0:T(1024)(128)(4,1)} %bitcast.183), calls=%async_computation.12 | async-start | bytes 8388608
  1332.1 8.2 slice-start.1
  1332.1 8.2 copy-start.20
  1431.5 12.8 copy-start.1
Sparse Core Ops, SparseCore 0:
  51.5 178.2 all-gather.8
  378.4 191.6 all-gather.10
  907.1 178.0 all-gather.12
  1210.5 149.1 all-gather.14
where the time goes:
time: 1460 us; the launch traced here: 1450 us
  waiting for transfers between devices  511 us (35%)
  local copies, waits for them, and re-layouts  333 us (23%)
  matrix products  180 us (12%)
  blocking collectives  146 us (10%)
  other arithmetic  145 us (10%)
  loops' own time  78.3 us (5%)
  starting transfers between devices  39.6 us (3%)
  between operations  18.6 us (1%)
    all_to_all x2, waiting for transfers between devices, run_block(): lax.all_to_all(normed, 'lon', split_axis=2, concat_axis=1, tiled=True)  181 us
    all_to_all x1, waiting for transfers between devices, run_block(): lax.all_to_all(synthesis, 'lat', split_axis=0, concat_axis=2, tiled=True)  128 us
    ppermute x1, waiting for transfers between devices, passed_along(): lax.ppermute(value, axis, [(source, source + steps) for source in range(l...  115 us
    convert_element_type x7, local copies, waits for them, and re-layouts, run_block(): mixed = base + spectral.astype(jnp.float32)  94 us
    all_to_all x2, waiting for transfers between devices, run_block(): lax.all_to_all(spectral, 'lon', split_axis=1, concat_axis=2, tiled=True)  86.5 us
    all_to_all x1, blocking collectives, run_block(): lax.all_to_all(spectrum, 'lat', split_axis=2, concat_axis=0, tiled=True)  80.7 us
    another operation x1, loops' own time, legendre_table(): lax.scan(advance, (jnp.zeros_like(start), jnp.zeros_like(start)), jnp.ara...  78.3 us
    dot_general x2, matrix products, run_block(): jnp.dot(flat, lax.all_gather(weight_in, 'lat', axis=0, tiled=True), prefe...  73.5 us
  transfers between devices with their start and end apart: 11, of which 6 were waited for; matrix products, arithmetic and copies ran while one was open for 33% of the time, Pallas kernels for 0%

commit v1 on v0

v1 whole, which is shorter than its diff:
```python
import functools
import math

import jax
import jax.numpy as jnp
from jax import lax
from jax.experimental import pallas as pl
from jax.experimental.pallas import tpu as pltpu
from jax.sharding import PartitionSpec as P


MM = 96
CHUNKS = 4

F32 = jnp.float32
BF16 = jnp.bfloat16
VMEM = 56 * 1024 * 1024


def chunks_of(n_rows):
    return CHUNKS if n_rows % CHUNKS == 0 else 1


def round_up(value, step):
    return (value + step - 1) // step * step


def exchange(values, axis):
    count = lax.axis_size(axis)
    got = [values[0]]
    for offset in range(1, count):
        pairs = [(s, (s + offset) % count) for s in range(count)]
        got.append(lax.ppermute(values[offset], axis, pairs))
    return got


def cost(flops, nbytes, trans=0):
    return pl.CostEstimate(flops=int(flops), bytes_accessed=int(nbytes), transcendentals=int(trans))


class Order:
    def __init__(self):
        self.last = []

    def call(self, kernel, operands, in_specs, **kwargs):
        deps = [d for d in self.last if all(d is not o for o in operands)]
        n_dep = len(deps)
        n_in = len(operands)

        def body(*refs):
            kernel(*refs[:n_in], *refs[n_in + n_dep :])

        outs = pl.pallas_call(
            body,
            in_specs=in_specs + [pl.BlockSpec(memory_space=pl.ANY)] * n_dep,
            compiler_params=params(),
            **kwargs,
        )(*operands, *deps)
        self.last = [outs[0]]
        return outs


def params(n_grid=1):
    return pltpu.CompilerParams(vmem_limit_bytes=VMEM, dimension_semantics=("arbitrary",) * n_grid)


def legendre_kernel(order_ref, cos_ref, start_ref, zero_ref, out_ref):
    order = order_ref[...]
    cosine = cos_ref[...]
    start = start_ref[...]
    zero = zero_ref[...]

    def advance(degree, carry):
        last, before = carry
        level = degree.astype(F32)
        coef_a = jnp.sqrt(
            jnp.maximum(4.0 * level * level - 1.0, 1.0)
            / jnp.maximum(level * level - order * order, 1.0)
        )
        coef_b = jnp.sqrt(
            jnp.maximum((level - 1.0) ** 2 - order * order, 0.0)
            / jnp.maximum(4.0 * (level - 1.0) ** 2 - 1.0, 1.0)
        )
        general = coef_a * (cosine * last - coef_b * before)
        row = jnp.where(level < order, zero, jnp.where(level == order, start, general))
        out_ref[degree] = row
        return (row, last)

    lax.fori_loop(0, out_ref.shape[0], advance, (zero, zero))


def legendre_table(orders, rows, n_rows, n_degrees):
    theta = math.pi * (rows.astype(F32) + 0.5) / n_rows
    cosine = jnp.cos(theta)
    sine = jnp.sin(theta)
    order = orders.astype(F32)[:, None]
    log_start = (
        0.5 * jnp.log((2.0 * order + 1.0) / (4.0 * math.pi))
        + jax.scipy.special.gammaln(order + 0.5)
        - jax.scipy.special.gammaln(0.5)
        - jax.scipy.special.gammaln(order + 1.0)
        + order * jnp.log(sine)[None, :]
    )
    start = jnp.exp(log_start)
    table = pl.pallas_call(
        legendre_kernel,
        out_shape=jax.ShapeDtypeStruct((n_degrees,) + start.shape, F32),
        name="legendre",
        cost_estimate=cost(1e6, 4 * n_degrees * start.size),
    )(jnp.broadcast_to(order, start.shape), jnp.broadcast_to(cosine[None, :], start.shape), start, jnp.zeros_like(start))
    quad = 2.0 * math.pi * (math.pi / n_rows) * sine
    return table, quad


def fourier_tables(n_lon):
    columns = jnp.arange(n_lon, dtype=jnp.int32)
    orders = jnp.arange(MM, dtype=jnp.int32)
    phase = 2.0 * math.pi * (columns[:, None] * orders[None, :] % n_lon).astype(F32) / n_lon
    weight = jnp.where(orders == 0, 1.0, 2.0).astype(F32)[None, :]
    forward = jnp.stack([jnp.cos(phase), -jnp.sin(phase)], 0) / n_lon
    inverse = jnp.stack([weight * jnp.cos(phase), -weight * jnp.sin(phase)], 0)
    return forward, inverse


def pick_tokens(flag_ref, tok_refs, row):
    if len(tok_refs) == 1:
        return tok_refs[0][row].astype(F32)
    return jnp.where(flag_ref[0] == 0, tok_refs[0][row].astype(F32), tok_refs[1][row].astype(F32))


def norm_rows(values, gain):
    center = values - jnp.mean(values, axis=-1, keepdims=True)
    spread = jnp.mean(center * center, axis=-1, keepdims=True)
    return center * lax.rsqrt(spread + 1e-05) * gain


def norm_kernel(n_tok, flag_ref, off_ref, *refs):
    tok_refs = refs[:n_tok]
    emb_ref, gain_ref = refs[n_tok : n_tok + 2]
    outs = refs[n_tok + 2 : -1]
    scr = refs[-1]
    cols = tok_refs[0].shape[1]
    part = outs[0].shape[-1]
    scr[...] = jnp.zeros_like(scr)

    def one(row, carry):
        x = pick_tokens(flag_ref, tok_refs, row) + emb_ref[...]
        scr[pl.ds(0, cols), :] = norm_rows(x, gain_ref[...]).astype(BF16)
        for o, out in enumerate(outs):
            out[row] = scr[:, pl.ds(pl.multiple_of(off_ref[o], 128), part)]
        return carry

    lax.fori_loop(0, tok_refs[0].shape[0], one, 0)


def dft_kernel(n_in, *refs):
    table_ref = refs[0]
    ins = refs[1 : 1 + n_in]
    outs = refs[1 + n_in :]
    height = outs[0].shape[1]

    def one(row, carry):
        wide = jnp.concatenate([r[row] for r in ins], axis=0)
        res = jnp.dot(table_ref[...], wide, preferred_element_type=F32).astype(BF16)
        for o, out in enumerate(outs):
            out[row] = res[o * height : (o + 1) * height]
        return carry

    lax.fori_loop(0, ins[0].shape[0], one, 0)


def spectral_kernel(n_in, m_local, *refs):
    ana_ref, syn_ref, filt_ref = refs[:3]
    ins = refs[3 : 3 + n_in]
    outs = refs[3 + n_in : 3 + 2 * n_in]
    scr = refs[-1]
    rows, height, width = ins[0].shape
    total = rows * n_in
    for p, ref in enumerate(ins):
        scr[pl.ds(p * rows * height, rows * height), :] = (
            ref[...].reshape(rows * height, width).astype(F32)
        )
    filt_re = filt_ref[0]
    filt_im = filt_ref[1]
    for m in range(m_local):
        at_re = pl.ds(m, total, stride=height)
        at_im = pl.ds(m_local + m, total, stride=height)
        both = jnp.concatenate([scr[at_re, :], scr[at_im, :]], axis=1).astype(BF16)
        coeff = jnp.dot(ana_ref[m], both, preferred_element_type=F32)
        c_re = coeff[:, :width]
        c_im = coeff[:, width:]
        out_re = c_re * filt_re - c_im * filt_im
        out_im = c_re * filt_im + c_im * filt_re
        filtered = jnp.concatenate([out_re, out_im], axis=1).astype(BF16)
        made = jnp.dot(syn_ref[m], filtered, preferred_element_type=F32)
        scr[at_re, :] = made[:, :width]
        scr[at_im, :] = made[:, width:]
    for p, ref in enumerate(outs):
        ref[...] = (
            scr[pl.ds(p * rows * height, rows * height), :].astype(BF16).reshape(rows, height, width)
        )


def gelu(x):
    inner = x * (0.7978845608028654 + 0.035677408136300125 * (x * x))
    half = 0.5 * x
    return half + half * jnp.tanh(inner)


def mlp_kernel(n_group, n_tok, n_lon, n_out, aliased, flag_ref, off_ref, *refs):
    n_all = n_group * n_tok
    tok_refs = [refs[g * n_tok : (g + 1) * n_tok] for g in range(n_group)]
    spec_refs = [refs[n_all + g * n_lon : n_all + (g + 1) * n_lon] for g in range(n_group)]
    base = n_all + n_group * n_lon
    emb_ref, gain_ref, win_ref, wout_ref = refs[base : base + 4]
    base += 5 if aliased else 4
    outs = refs[base : base + n_out]
    acc, n2, spec = refs[base + n_out :]
    rows, cols, width = tok_refs[0][0].shape
    part = spec_refs[0][0].shape[-1]
    height = acc.shape[0]
    block_f = win_ref.shape[-1]
    step = pl.program_id(0)

    @pl.when(step == 0)
    def _():
        used = n_group * rows * cols
        if height > used:
            tail = used // 8 * 8
            acc[pl.ds(tail, height - tail), :] = jnp.zeros((height - tail, width), F32)
        for g in range(n_group):
            for row in range(rows):
                for o, ref in enumerate(spec_refs[g]):
                    spec[:, pl.ds(pl.multiple_of(off_ref[o], 128), part)] = ref[row]
                u = pick_tokens(flag_ref, tok_refs[g], row) + emb_ref[...]
                at = pl.ds((g * rows + row) * cols, cols)
                acc[at, :] = u + spec[pl.ds(0, cols), :].astype(F32)

        def norm_block(i, carry):
            at = pl.ds(pl.multiple_of(i * 128, 128), 128)
            n2[at, :] = norm_rows(acc[at, :], gain_ref[...]).astype(BF16)
            return carry

        lax.fori_loop(0, height // 128, norm_block, 0)

    tile = 640 if height % 640 == 0 else 128
    for i in range(height // tile):
        at = pl.ds(i * tile, tile)
        weight_in = win_ref[...].reshape(width, block_f)
        weight_out = wout_ref[...].reshape(width, block_f)
        pre = jnp.dot(n2[at, :], weight_in, preferred_element_type=F32)
        hidden = gelu(pre).astype(BF16)
        acc[at, :] += lax.dot_general(
            hidden, weight_out, (((1,), (1,)), ((), ())), preferred_element_type=F32
        )

    @pl.when(step == pl.num_programs(0) - 1)
    def _():
        for row in range(n_group * rows):
            value = acc[pl.ds(row * cols, cols), :].astype(BF16)
            for out in outs:
                if len(out.shape) == 3:
                    out[row] = value
                else:
                    out[0, row] = value


def local(state, fresh, cutoff, plan, lmax, mmax, cutoff_table, norm_gains, filters, w_in, w_out):
    section_idx = lax.axis_index("section")
    lat_idx = lax.axis_index("lat")
    lon_idx = lax.axis_index("lon")
    n_section = lax.axis_size("section")
    n_lat = lax.axis_size("lat")
    n_lon = lax.axis_size("lon")
    n_rows, n_cols, width = fresh.shape
    n_degrees = filters.shape[3]
    ff = w_in.shape[3]
    part = width // n_lon
    all_rows = n_rows * n_lat
    all_cols = n_cols * n_lon
    m_local = MM // n_lat
    height = round_up(2 * m_local, 16)
    cols_pad = round_up(n_cols, 16)
    n_chunk = chunks_of(n_rows)
    rows = n_rows // n_chunk

    lon_fwd = (lon_idx + jnp.arange(n_lon, dtype=jnp.int32)) % n_lon
    lon_bwd = (lon_idx - jnp.arange(n_lon, dtype=jnp.int32)) % n_lon
    lat_fwd = (lat_idx + jnp.arange(n_lat, dtype=jnp.int32)) % n_lat
    lat_bwd = (lat_idx - jnp.arange(n_lat, dtype=jnp.int32)) % n_lat
    off_fwd = lon_fwd * part
    off_bwd = lon_bwd * part

    def gathered(tick):
        block = plan[tick, section_idx]
        local_rows = w_in.shape[2]
        piece = ff // n_lon
        start = (0, block, 0, lon_idx * piece)
        size = (1, 1, local_rows, piece)
        mine = jnp.concatenate(
            [lax.dynamic_slice(w_in, start, size)[0], lax.dynamic_slice(w_out, start, size)[0]], 0
        )
        rows_here = lax.all_gather(mine, "lat")
        return lax.all_gather(rows_here, "lon")

    weights = [gathered(t) for t in range(2)]

    forward, inverse = fourier_tables(all_cols)

    def modes(table, order):
        t = table.transpose(2, 0, 1).reshape(n_lat, m_local, 2, all_cols).transpose(0, 2, 1, 3)
        t = t.reshape(n_lat, 2 * m_local, all_cols)[order]
        return jnp.pad(t, ((0, 0), (0, height - 2 * m_local), (0, 0)))

    def columns(table, order):
        t = table.reshape(n_lat, height, n_lon, n_cols)[:, :, order]
        t = jnp.pad(t, ((0, 0), (0, 0), (0, 0), (0, cols_pad - n_cols)))
        return t.reshape(n_lat * height, n_lon * cols_pad)

    dft = columns(modes(forward, lat_fwd), lon_bwd).astype(BF16)
    idft = columns(modes(inverse, lat_bwd), lon_fwd).T.astype(BF16)

    orders = lat_idx * m_local + jnp.arange(m_local, dtype=jnp.int32)
    row_ids = (lat_bwd[:, None] * n_rows + jnp.arange(n_rows, dtype=jnp.int32)[None, :]).reshape(-1)
    table, quad = legendre_table(orders, row_ids, all_rows, n_degrees)
    m_max = mmax[section_idx]
    l_max = lmax[section_idx]
    ana = (table * quad[None, None, :]).astype(BF16).transpose(1, 0, 2)
    keep_m = (orders < m_max).astype(F32)
    syn = (table * keep_m[None, :, None]).astype(BF16).transpose(1, 2, 0)
    back = [(n_lat - o) % n_lat for o in range(n_lat)]
    syn = syn.reshape(m_local, n_lat, n_rows, n_degrees)
    syn = jnp.concatenate([syn[:, b : b + 1] for b in back], 1).reshape(m_local, all_rows, n_degrees)
    keep_l = (jnp.arange(n_degrees, dtype=jnp.int32) < l_max)[None, :, None]

    smem = pl.BlockSpec(memory_space=pltpu.SMEM)
    whole = pl.BlockSpec(memory_space=pltpu.VMEM)
    flag = section_idx.astype(jnp.int32).reshape(1)
    token_block = (rows, n_cols, width)

    def token_specs(tokens, chunk):
        specs = []
        for t in tokens:
            if t.shape[0] == rows and n_chunk > 1:
                specs.append(pl.BlockSpec(token_block, lambda *_: (0, 0, 0)))
            else:
                specs.append(pl.BlockSpec(token_block, lambda *_, c=chunk: (c, 0, 0)))
        return specs

    order = Order()

    def norm_call(tokens, chunk, emb, gain):
        piece = jax.ShapeDtypeStruct((rows, cols_pad, part), BF16)
        return order.call(
            functools.partial(norm_kernel, len(tokens)),
            [flag, off_fwd, *tokens, emb, gain],
            [smem, smem] + token_specs(tokens, chunk) + [whole, whole],
            grid=(1,),
            out_specs=[pl.BlockSpec((rows, cols_pad, part), lambda i: (0, 0, 0))] * n_lon,
            out_shape=[piece] * n_lon,
            scratch_shapes=[pltpu.VMEM((cols_pad, width), BF16)],
            name="norm",
            cost_estimate=cost(4e9 / n_chunk, 4 * rows * n_cols * width),
        )

    def table_call(table, pieces, n_out, out_height, name):
        r, h, c = pieces[0].shape
        return order.call(
            functools.partial(dft_kernel, len(pieces)),
            [table, *pieces],
            [whole] * (1 + len(pieces)),
            grid=(1,),
            out_specs=[whole] * n_out,
            out_shape=[jax.ShapeDtypeStruct((r, out_height, c), BF16)] * n_out,
            name=name,
            cost_estimate=cost(4 * table.size * c * r, 4 * r * h * c * len(pieces)),
        )

    def spectral_call(pieces, filt):
        n_in = len(pieces)
        half = 128 if part % 128 == 0 else part
        tables = pl.BlockSpec(memory_space=pltpu.VMEM)
        block = pl.BlockSpec((rows, height, half), lambda i: (0, 0, i))
        return order.call(
            functools.partial(spectral_kernel, n_in, m_local),
            [ana, syn, filt, *pieces],
            [tables, tables, pl.BlockSpec((2, n_degrees, half), lambda i: (0, 0, i))]
            + [block] * n_in,
            grid=(part // half,),
            out_specs=[block] * n_in,
            out_shape=[jax.ShapeDtypeStruct((rows, height, part), BF16)] * n_in,
            scratch_shapes=[pltpu.VMEM((all_rows * height, half), F32)],
            name="spectral",
            cost_estimate=cost(8e9, 8e6),
        )

    def mlp_call(chunks, tokens, spec, emb, gain, weight, full, want_chunk):
        n_group = len(chunks)
        block_f = min(512, ff // n_lon)
        per = ff // n_lon // block_f
        m_pad = round_up(n_group * rows * n_cols, 128)
        n_tok = len(tokens[0])
        chunk_shape = jax.ShapeDtypeStruct(token_block, BF16)
        full_shape = jax.ShapeDtypeStruct((1, n_rows, n_cols, width), BF16)
        out_shape = [full_shape] + ([chunk_shape] if want_chunk else [])
        at = chunks[0] // n_group
        out_specs = [
            pl.BlockSpec((1, n_group * rows, n_cols, width), lambda i, at=at: (0, at, 0, 0))
        ]
        if want_chunk:
            out_specs.append(pl.BlockSpec(token_block, lambda i: (0, 0, 0)))
        block = (None, n_lat, None, weight.shape[3], block_f)
        in_specs = [smem, smem]
        for c, t in zip(chunks, tokens):
            in_specs += token_specs(t, c)
        in_specs += [whole] * (n_group * n_lon + 2)
        in_specs += [
            pl.BlockSpec(block, lambda i: (i // per, 0, 0, 0, i % per)),
            pl.BlockSpec(block, lambda i: (i // per, 0, 1, 0, i % per)),
        ]
        args = [flag, off_bwd]
        for t in tokens:
            args += t
        for s in spec:
            args += s
        args += [emb, gain, weight, weight]
        aliases = {}
        if full is not None:
            in_specs.append(pl.BlockSpec(memory_space=pl.ANY))
            aliases = {len(args): 0}
            args.append(full)
        return order.call(
            functools.partial(mlp_kernel, n_group, n_tok, n_lon, len(out_shape), full is not None),
            args,
            in_specs,
            grid=(ff // block_f,),
            out_specs=out_specs,
            out_shape=out_shape,
            scratch_shapes=[
                pltpu.VMEM((m_pad, width), F32),
                pltpu.VMEM((m_pad, width), BF16),
                pltpu.VMEM((cols_pad, width), BF16),
            ],
            input_output_aliases=aliases,
            name="mlp",
            cost_estimate=cost(4 * m_pad * width * ff, 4 * width * ff, m_pad * ff),
        )

    def settings(tick):
        block = plan[tick, section_idx]
        cut = cutoff[tick - section_idx + n_section - 1]
        gains = norm_gains[0, block]
        filt = jnp.where(keep_l, filters[0, block], 0.0)
        emb = cutoff_table[cut][None, :]
        return emb, gains[0:1], gains[1:2], filt

    pass_on = [(s, s + 1) for s in range(n_section - 1)]
    ticks = [settings(0), settings(1)]
    tokens = [[[state[0]]] * n_chunk, [None] * n_chunk]
    lonf, latf, latb, lonb = {}, {}, {}, {}
    full = [None, None]

    def do_norm(t, c):
        emb, gain_a, _, _ = ticks[t]
        sent = norm_call(tokens[t][c], c, emb, gain_a)
        lonf[t, c] = exchange(sent, "lon")

    def do_dft(t, c):
        made = table_call(dft, lonf[t, c], n_lat, height, "dft")
        latf[t, c] = exchange(made, "lat")

    def do_spectral(t):
        pieces = [latf[t, c][o] for o in range(n_lat) for c in range(n_chunk)]
        made = spectral_call(pieces, ticks[t][3])
        for c in range(n_chunk):
            latb[t, c] = exchange([made[o * n_chunk + c] for o in range(n_lat)], "lat")

    def do_idft(t, c):
        made = table_call(idft, latb[t, c], n_lon, cols_pad, "idft")
        lonb[t, c] = exchange(made, "lon")

    def do_mlp(t, c):
        emb, _, gain_b, _ = ticks[t]
        group = [c] if t == 0 or n_chunk % 2 else [c, c + 1]
        outs = mlp_call(
            group, [tokens[t][g] for g in group], [lonb[t, g] for g in group],
            emb, gain_b, weights[t], full[t], t == 0,
        )
        full[t] = outs[0]
        if t == 0:
            handed = lax.ppermute(outs[1], "section", pass_on)
            tokens[1][c] = [fresh, handed]

    steps = {"N": do_norm, "D": do_dft, "S": lambda t, c: do_spectral(t), "I": do_idft, "M": do_mlp}
    for kind, t, c in kernel_order(n_chunk):
        if (kind, t, c) == ("D", 0, n_chunk // 3):
            order.last = order.last + [ana, syn]
        steps[kind](t, c)
    return (full[0], full[1])


def kernel_order(n_chunk):
    if n_chunk == 4:
        text = (
            "N00 N01 N02 N03",
            "D00 D01 D02 D03",
            "S00 I00 I01 M00",
            "I02 M01 N10 I03",
            "M02 N11 D10 M03",
            "N12 D11 N13 D12",
            "D13 S10 I10 I11",
            "I12 I13 M10 M12",
        )
        return [(w[0], int(w[1]), int(w[2])) for w in " ".join(text).split()]
    every = range(n_chunk)
    order = []
    for t in range(2):
        order += [("N", t, c) for c in every] + [("D", t, c) for c in every] + [("S", t, 0)]
        order += [("I", t, c) for c in every] + [("M", t, c) for c in every]
    return order


def solution(mesh):
    return jax.shard_map(
        local,
        mesh=mesh,
        in_specs=(
            P("section", "lat", "lon", None),
            P("lat", "lon", None),
            P(),
            P(),
            P(),
            P(),
            P(),
            P("section", None, None, None),
            P("section", None, None, None, "lon"),
            P("section", None, "lat", None),
            P("section", None, "lat", None),
        ),
        out_specs=(P("section", "lat", "lon", None), P("section", "lat", "lon", None)),
        check_vma=False,
    )
```

time: 1460 us -> 880 us (0.60)
  local copies, waits for them, and re-layouts: 333 us -> 28.2 us
  Pallas kernels: 0 us -> 270 us
  matrix products: 180 us -> 0 us
  waiting for transfers between devices: 511 us -> 344 us
  starting transfers between devices: 39.6 us -> 194 us
  blocking collectives: 146 us -> 0 us
  other arithmetic: 145 us -> 11.1 us
  loops' own time: 78.3 us -> 0 us
    all_to_all x6 -> x0, waiting for transfers between devices: 395 us -> none  [the longest x2 181 us: run_block(): lax.all_to_all(normed, 'lon', split_axis=2, concat_axis=1, tiled=True)]
    pallas_call x0 -> x33, Pallas kernels: none -> 270 us  [the longest x32 265 us: call(): pl.pallas_call(body, in_specs=in_specs + [pl.BlockSpec(memory_space=pl.AN...]
    ppermute x1 -> x100, starting transfers between devices: 5.78 us -> 194 us  [the longest x96 184 us: exchange(): got.append(lax.ppermute(values[offset], axis, pairs))]
    dot_general x16 -> x0, matrix products: 180 us -> none  [the longest x2 73.5 us: run_block(): jnp.dot(flat, lax.all_gather(weight_in, 'lat', axis=0, tiled=True), prefe...]
    all_gather x4, waiting for transfers between devices: 0.01 us -> 164 us  [the longest x2 164 us: gathered(): rows_here = lax.all_gather(mine, 'lat')]
    all_to_all x2 -> x0, blocking collectives: 146 us -> none  [the longest x1 80.7 us: run_block(): lax.all_to_all(spectrum, 'lat', split_axis=2, concat_axis=0, tiled=True)]
    convert_element_type x14 -> x2, local copies, waits for them, and re-layouts: 140 us -> 1.74 us  [the longest x1 0.91 us: local(): idft = columns(modes(inverse, lat_bwd), lon_fwd).T.astype(BF16)]
    another operation x1 -> x0, loops' own time: 78.3 us -> none  [legendre_table(): lax.scan(advance, (jnp.zeros_like(start), jnp.zeros_like(start)), jnp.ara...]
  transfers between devices with their start and end apart: 11 -> 104, of which waited for: 6 -> 38; matrix products, arithmetic and copies ran while one was open for 33% -> 3% of each run, Pallas kernels for 0% -> 27%
where the time goes in v1:
time: 880 us; the launch traced here: 870 us
  waiting for transfers between devices  344 us (39%)
  Pallas kernels  270 us (31%)
  starting transfers between devices  194 us (22%)
  local copies, waits for them, and re-layouts  28.2 us (3%)
  between operations  23 us (3%)
  other arithmetic  11.1 us (1%)
    pallas_call x32, Pallas kernels, call(): pl.pallas_call(body, in_specs=in_specs + [pl.BlockSpec(memory_space=pl.AN...  265 us
    ppermute x96, starting transfers between devices, exchange(): got.append(lax.ppermute(values[offset], axis, pairs))  184 us
    ppermute x96, waiting for transfers between devices, exchange(): got.append(lax.ppermute(values[offset], axis, pairs))  168 us
    all_gather x2, waiting for transfers between devices, gathered(): rows_here = lax.all_gather(mine, 'lat')  164 us
  transfers between devices with their start and end apart: 104, of which 38 were waited for; matrix products, arithmetic and copies ran while one was open for 3% of the time, Pallas kernels for 27%

profile of v1, /device:TPU:0, one launch (start us, length us, event | category | flops | bytes accessed | tf_op | source)
XLA Modules:
  0.0 870.3 jit_solution(17497254259209059571)
XLA Ops:
  16.5 82.4 %all-gather.9.cloned.1.call-done = bf16[8,256,1024]{2,1,0:T(8,128)(2,1)} async-done(((bf16[2,256,1024]{2,1,0:T(8,128)(2,1)}), bf16[8,256,1024]{2,1,0:T(8,128)(2,1)}) %all-gather.9.cloned.1.call-update) | async-done | bytes 4194320 | tf_op jit(solution)/shard_map/all_gather | solution.py:303
  99.0 81.3 %all-gather.13.cloned.1.call-done = bf16[8,256,1024]{2,1,0:T(8,128)(2,1)} async-done(((bf16[2,256,1024]{2,1,0:T(8,128)(2,1)}), bf16[8,256,1024]{2,1,0:T(8,128)(2,1)}) %all-gather.13.cloned.1.call-update) | async-done | bytes 4194320 | tf_op jit(solution)/shard_map/all_gather | solution.py:303
  194.7 4.7 norm.9
  203.2 4.9 legendre.1
  219.2 5.1 collective-permute-start.6
  227.3 11.5 %collective-permute-done.3.refs_2_ = bf16[7,96,256]{2,1,0:T(8,128)(2,1)S(1)} collective-permute-done((bf16[7,96,256]{2,1,0:T(8,128)(2,1)}, bf16[7,96,256]{2,1,0:T(8,128)(2,1)S(1)}, u32[]{:S(2)}, u32[]{:S(2)}) %collective-permute-start.3) | collective-permute-done | bytes 344096 | tf_op jit(solution)/shard_map/ppermute | solution.py:33
  248.5 5.2 collective-permute-done.5.refs_4_
  255.9 12.4 %collective-permute-done.6.refs_2_ = bf16[7,96,256]{2,1,0:T(8,128)(2,1)S(1)} collective-permute-done((bf16[7,96,256]{2,1,0:T(8,128)(2,1)}, bf16[7,96,256]{2,1,0:T(8,128)(2,1)S(1)}, u32[]{:S(2)}, u32[]{:S(2)}) %collective-permute-start.6) | collective-permute-done | bytes 344096 | tf_op jit(solution)/shard_map/ppermute | solution.py:33
  276.6 6.6 collective-permute-done.8.refs_4_
  286.8 12.0 %collective-permute-done.10.refs_3_ = bf16[7,96,256]{2,1,0:T(8,128)(2,1)S(1)} collective-permute-done((bf16[7,96,256]{2,1,0:T(8,128)(2,1)}, bf16[7,96,256]{2,1,0:T(8,128)(2,1)S(1)}, u32[]{:S(2)}, u32[]{:S(2)}) %collective-permute-start.10) | collective-permute-done | bytes 344096 | tf_op jit(solution)/shard_map/ppermute | solution.py:33
  298.8 13.7 %collective-permute-done.11.refs_4_ = bf16[7,96,256]{2,1,0:T(8,128)(2,1)S(1)} collective-permute-done((bf16[7,96,256]{2,1,0:T(8,128)(2,1)}, bf16[7,96,256]{2,1,0:T(8,128)(2,1)S(1)}, u32[]{:S(2)}, u32[]{:S(2)}) %collective-permute-start.11) | collective-permute-done | bytes 344096 | tf_op jit(solution)/shard_map/ppermute | solution.py:33
  326.4 6.4 collective-permute-done.19.refs_14_
  335.0 8.5 collective-permute-start.17
  346.8 8.2 collective-permute-done.18.refs_13_
  361.7 8.0 collective-permute-done.17.refs_12_
  369.7 7.3 collective-permute-done.16.refs_11_
  377.8 7.1 spectral.2
  397.5 4.6 collective-permute-done.28.refs_3_
  409.8 6.0 collective-permute-start.35
  416.0 4.9 collective-permute-start.40
  421.4 4.7 collective-permute-done.35.refs_4_
  426.1 5.4 collective-permute-start.41
  441.5 20.3 %mlp.6 = (bf16[1,28,90,1024]{3,2,1,0:T(8,128)(2,1)}, bf16[7,90,1024]{2,1,0:T(8,128)(2,1)}) custom-call(s32[1]{0:T(128)} %bitcast.refs_0_, s32[4]{0:T(128)} %fusion.16.refs_1_, bf16[28,90,1024]{2,1,0:T(8,128)(2,1)} %bitcast.79, bf16[7,96,256]{2,1,0:T(8,128)(2,1)} %get-tuple-element.178.refs_5_.refs_3_, bf16[7,96,256]{2,1,0:T(8,128)(2,1)} %copy-done.15, ...), custom_call_target="tpu_custom_call" | custom-call | flops 10737418240 | bytes 16777216 | tf_op jit(solution)/shard_map/mlp/pallas_call | solution.py:53
  471.5 20.2 %mlp.7 = (bf16[1,28,90,1024]{3,2,1,0:T(8,128)(2,1)}, bf16[7,90,1024]{2,1,0:T(8,128)(2,1)}) custom-call(s32[1]{0:T(128)} %bitcast.refs_0_, s32[4]{0:T(128)} %fusion.16.refs_1_, bf16[28,90,1024]{2,1,0:T(8,128)(2,1)} %bitcast.80, bf16[7,96,256]{2,1,0:T(8,128)(2,1)} %get-tuple-element.186.refs_11_.refs_3_, ...), custom_call_target="tpu_custom_call", output_to_operand_aliasing={{0}: (11, {})} | custom-call | flops 10737418240 | bytes 16777216 | tf_op jit(solution)/shard_map/mlp/pallas_call | solution.py:53
  495.3 7.9 collective-permute-start.24
  508.6 6.4 collective-permute-done.25.refs_3_
  517.0 4.8 norm.12
  534.1 20.1 %mlp.8 = (bf16[1,28,90,1024]{3,2,1,0:T(8,128)(2,1)}, bf16[7,90,1024]{2,1,0:T(8,128)(2,1)}) custom-call(s32[1]{0:T(128)} %bitcast.refs_0_, s32[4]{0:T(128)} %fusion.16.refs_1_, bf16[28,90,1024]{2,1,0:T(8,128)(2,1)} %bitcast.81, bf16[7,96,256]{2,1,0:T(8,128)(2,1)} %get-tuple-element.196.refs_12_.refs_3_, ...), custom_call_target="tpu_custom_call", output_to_operand_aliasing={{0}: (11, {})} | custom-call | flops 10737418240 | bytes 16777216 | tf_op jit(solution)/shard_map/mlp/pallas_call | solution.py:53
  554.2 4.9 norm.13
  565.8 20.2 %mlp.9 = (bf16[1,28,90,1024]{3,2,1,0:T(8,128)(2,1)}, bf16[7,90,1024]{2,1,0:T(8,128)(2,1)}) custom-call(s32[1]{0:T(128)} %bitcast.refs_0_, s32[4]{0:T(128)} %fusion.16.refs_1_, bf16[28,90,1024]{2,1,0:T(8,128)(2,1)} %bitcast.82, bf16[7,96,256]{2,1,0:T(8,128)(2,1)} %get-tuple-element.199.refs_12_.refs_3_, ...), custom_call_target="tpu_custom_call", output_to_operand_aliasing={{0}: (11, {})} | custom-call | flops 10737418240 | bytes 16777216 | tf_op jit(solution)/shard_map/mlp/pallas_call | solution.py:53
  592.1 4.8 norm.14
  598.5 5.8 collective-permute-start.60
  608.8 10.8 %collective-permute-done.54.refs_3_.refs_5_ = bf16[7,90,1024]{2,1,0:T(8,128)(2,1)S(1)} collective-permute-done((bf16[7,90,1024]{2,1,0:T(8,128)(2,1)}, bf16[7,90,1024]{2,1,0:T(8,128)(2,1)S(1)}, u32[]{:S(2)}, u32[]{:S(2)}) %collective-permute-start.54) | collective-permute-done | bytes 1290272 | tf_op jit(solution)/shard_map/ppermute | solution.py:491
  620.8 4.8 norm.15
  628.4 5.8 collective-permute-start.64
  642.3 4.7 collective-permute-done.68.refs_11_
  662.0 5.2 collective-permute-done.69.refs_12_
  667.3 7.7 collective-permute-start.71
  678.3 6.3 collective-permute-done.70.refs_13_
  684.7 7.3 collective-permute-done.71.refs_14_
  692.7 7.2 spectral.3
  710.4 6.2 collective-permute-done.83.refs_3_
  720.1 6.9 collective-permute-start.77
  757.1 6.5 collective-permute-done.89.refs_3_
  774.9 5.9 collective-permute-start.85
  781.8 6.5 collective-permute-done.91.refs_11_
  788.4 37.0 %mlp.10.refs_18_ = bf16[1,28,90,1024]{3,2,1,0:T(8,128)(2,1)} custom-call(s32[1]{0:T(128)} %bitcast.refs_0_, s32[4]{0:T(128)} %fusion.16.refs_1_, bf16[28,90,1024]{2,1,0:T(8,128)(2,1)} %refs_4_.3, bf16[7,90,1024]{2,1,0:T(8,128)(2,1)} %copy-done.1, bf16[28,90,1024]{2,1,0:T(8,128)(2,1)} %refs_4_.3, bf16[7,90,1024]{2,1,0:T(8,128)(2,1)} %copy-done.2, ...), custom_call_target="tpu_custom_call" | custom-call | flops 21474836480 | bytes 16777216 | tf_op jit(solution)/shard_map/mlp/pallas_call | solution.py:53
  826.4 36.9 %mlp.11 = bf16[1,28,90,1024]{3,2,1,0:T(8,128)(2,1)} custom-call(s32[1]{0:T(128)} %bitcast.refs_0_, s32[4]{0:T(128)} %fusion.16.refs_1_, bf16[28,90,1024]{2,1,0:T(8,128)(2,1)} %refs_4_.3, bf16[7,90,1024]{2,1,0:T(8,128)(2,1)} %copy-done.3, bf16[28,90,1024]{2,1,0:T(8,128)(2,1)} %refs_4_.3, ...), custom_call_target="tpu_custom_call", output_to_operand_aliasing={{}: (18, {})} | custom-call | flops 21474836480 | bytes 16777216 | tf_op jit(solution)/shard_map/mlp/pallas_call | solution.py:53
  (501 shorter events, 255.0 us)
Async XLA Ops:
  7.2 91.7 %all-gather.9.cloned.1.call-start = ((), (), s32[]{:S(2)}) async-start(), calls=%async_computation | async-start | bytes 5242880 | tf_op jit(solution)/shard_map/all_gather | solution.py:303
  15.3 165.0 %all-gather.13.cloned.1.call-start = ((), (), s32[]{:S(2)}) async-start(), calls=%async_computation.2 | async-start | bytes 5242880 | tf_op jit(solution)/shard_map/all_gather | solution.py:303
  16.4 425.1 %all-gather.11.cloned.1.call-start = ((), (), s32[]{:S(2)}) async-start(), calls=%async_computation.1 | async-start | bytes 20971520 | tf_op jit(solution)/shard_map/all_gather | solution.py:304
  98.9 689.4 %all-gather.15.cloned.1.call-start = ((), (), s32[]{:S(2)}) async-start(), calls=%async_computation.3 | async-start | bytes 20971520 | tf_op jit(solution)/shard_map/all_gather | solution.py:304
  191.8 27.4 %collective-permute-start.1 = (bf16[7,96,256]{2,1,0:T(8,128)(2,1)}, bf16[7,96,256]{2,1,0:T(8,128)(2,1)}, u32[]{:S(2)}, u32[]{:S(2)}) collective-permute-start(bf16[7,96,256]{2,1,0:T(8,128)(2,1)} %get-tuple-element.140), channel_id=1, source_target_pairs={{0,2},{1,3},{2,0},{3,1},{4,6},{5,7},{6,4},{7,5},{8,10},{9,11},{10,... | collective-permute-start | bytes 1032200 | tf_op jit(solution)/shard_map/ppermute | solution.py:33
  193.3 32.1 %collective-permute-start.2 = (bf16[7,96,256]{2,1,0:T(8,128)(2,1)}, bf16[7,96,256]{2,1,0:T(8,128)(2,1)}, u32[]{:S(2)}, u32[]{:S(2)}) collective-permute-start(bf16[7,96,256]{2,1,0:T(8,128)(2,1)} %get-tuple-element.141), channel_id=1, source_target_pairs={{0,3},{1,0},{2,1},{3,2},{4,7},{5,4},{6,5},{7,6},{8,11},{9,8},{10,9... | collective-permute-start | bytes 1032200 | tf_op jit(solution)/shard_map/ppermute | solution.py:33
  199.4 39.4 %collective-permute-start.3 = (bf16[7,96,256]{2,1,0:T(8,128)(2,1)}, bf16[7,96,256]{2,1,0:T(8,128)(2,1)S(1)}, u32[]{:S(2)}, u32[]{:S(2)}) collective-permute-start(bf16[7,96,256]{2,1,0:T(8,128)(2,1)} %get-tuple-element.146), channel_id=1, source_target_pairs={{0,1},{1,2},{2,3},{3,0},{4,5},{5,6},{6,7},{7,4},{8,9},{9,10},{10,1... | collective-permute-start | bytes 1032200 | tf_op jit(solution)/shard_map/ppermute | solution.py:33
  199.4 47.2 %collective-permute-start.4 = (bf16[7,96,256]{2,1,0:T(8,128)(2,1)}, bf16[7,96,256]{2,1,0:T(8,128)(2,1)S(1)}, u32[]{:S(2)}, u32[]{:S(2)}) collective-permute-start(bf16[7,96,256]{2,1,0:T(8,128)(2,1)} %get-tuple-element.147), channel_id=1, source_target_pairs={{0,2},{1,3},{2,0},{3,1},{4,6},{5,7},{6,4},{7,5},{8,10},{9,11},{10,... | collective-permute-start | bytes 1032200 | tf_op jit(solution)/shard_map/ppermute | solution.py:33
  217.6 36.1 %collective-permute-start.5 = (bf16[7,96,256]{2,1,0:T(8,128)(2,1)}, bf16[7,96,256]{2,1,0:T(8,128)(2,1)S(1)}, u32[]{:S(2)}, u32[]{:S(2)}) collective-permute-start(bf16[7,96,256]{2,1,0:T(8,128)(2,1)} %get-tuple-element.148), channel_id=1, source_target_pairs={{0,3},{1,0},{2,1},{3,2},{4,7},{5,4},{6,5},{7,6},{8,11},{9,8},{10,9... | collective-permute-start | bytes 1032200 | tf_op jit(solution)/shard_map/ppermute | solution.py:33
  219.2 49.1 %collective-permute-start.6 = (bf16[7,96,256]{2,1,0:T(8,128)(2,1)}, bf16[7,96,256]{2,1,0:T(8,128)(2,1)S(1)}, u32[]{:S(2)}, u32[]{:S(2)}) collective-permute-start(bf16[7,96,256]{2,1,0:T(8,128)(2,1)} %get-tuple-element.150), channel_id=1, source_target_pairs={{0,1},{1,2},{2,3},{3,0},{4,5},{5,6},{6,7},{7,4},{8,9},{9,10},{10,1... | collective-permute-start | bytes 1032200 | tf_op jit(solution)/shard_map/ppermute | solution.py:33
  225.4 51.2 %collective-permute-start.7 = (bf16[7,96,256]{2,1,0:T(8,128)(2,1)}, bf16[7,96,256]{2,1,0:T(8,128)(2,1)}, u32[]{:S(2)}, u32[]{:S(2)}) collective-permute-start(bf16[7,96,256]{2,1,0:T(8,128)(2,1)} %get-tuple-element.151), channel_id=1, source_target_pairs={{0,2},{1,3},{2,0},{3,1},{4,6},{5,7},{6,4},{7,5},{8,10},{9,11},{10,... | collective-permute-start | bytes 1032200 | tf_op jit(solution)/shard_map/ppermute | solution.py:33
  238.8 44.4 %collective-permute-start.8 = (bf16[7,96,256]{2,1,0:T(8,128)(2,1)}, bf16[7,96,256]{2,1,0:T(8,128)(2,1)}, u32[]{:S(2)}, u32[]{:S(2)}) collective-permute-start(bf16[7,96,256]{2,1,0:T(8,128)(2,1)} %get-tuple-element.152), channel_id=1, source_target_pairs={{0,3},{1,0},{2,1},{3,2},{4,7},{5,4},{6,5},{7,6},{8,11},{9,8},{10,9... | collective-permute-start | bytes 1032200 | tf_op jit(solution)/shard_map/ppermute | solution.py:33
  246.6 52.2 %collective-permute-start.10 = (bf16[7,96,256]{2,1,0:T(8,128)(2,1)}, bf16[7,96,256]{2,1,0:T(8,128)(2,1)S(1)}, u32[]{:S(2)}, u32[]{:S(2)}) collective-permute-start(bf16[7,96,256]{2,1,0:T(8,128)(2,1)} %get-tuple-element.155), channel_id=1, source_target_pairs={{0,2},{1,3},{2,0},{3,1},{4,6},{5,7},{6,4},{7,5},{8,10},{9,11},{10,... | collective-permute-start | bytes 1032200 | tf_op jit(solution)/shard_map/ppermute | solution.py:33
  253.7 58.8 %collective-permute-start.11 = (bf16[7,96,256]{2,1,0:T(8,128)(2,1)}, bf16[7,96,256]{2,1,0:T(8,128)(2,1)S(1)}, u32[]{:S(2)}, u32[]{:S(2)}) collective-permute-start(bf16[7,96,256]{2,1,0:T(8,128)(2,1)} %get-tuple-element.156), channel_id=1, source_target_pairs={{0,3},{1,0},{2,1},{3,2},{4,7},{5,4},{6,5},{7,6},{8,11},{9,8},{10,9... | collective-permute-start | bytes 1032200 | tf_op jit(solution)/shard_map/ppermute | solution.py:33
  268.3 44.3 %collective-permute-start.9 = (bf16[7,96,256]{2,1,0:T(8,128)(2,1)}, bf16[7,96,256]{2,1,0:T(8,128)(2,1)S(1)}, u32[]{:S(2)}, u32[]{:S(2)}) collective-permute-start(bf16[7,96,256]{2,1,0:T(8,128)(2,1)} %get-tuple-element.154), channel_id=1, source_target_pairs={{0,1},{1,2},{2,3},{3,0},{4,5},{5,6},{6,7},{7,4},{8,9},{9,10},{10,1... | collective-permute-start | bytes 1032200 | tf_op jit(solution)/shard_map/ppermute | solution.py:33
  322.1 32.8 %collective-permute-start.18 = (bf16[7,48,256]{2,1,0:T(8,128)(2,1)}, bf16[7,48,256]{2,1,0:T(8,128)(2,1)S(1)}, u32[]{:S(2)}, u32[]{:S(2)}) collective-permute-start(bf16[7,48,256]{2,1,0:T(8,128)(2,1)} %get-tuple-element.164), channel_id=1, source_target_pairs={{0,8},{4,12},{8,0},{12,4},{1,9},{5,13},{9,1},{13,5},{2,10},{6,14},... | collective-permute-start | bytes 516104 | tf_op jit(solution)/shard_map/ppermute | solution.py:33
  326.4 30.1 %collective-permute-start.22 = (bf16[7,48,256]{2,1,0:T(8,128)(2,1)}, bf16[7,48,256]{2,1,0:T(8,128)(2,1)S(1)}, u32[]{:S(2)}, u32[]{:S(2)}) collective-permute-start(bf16[7,48,256]{2,1,0:T(8,128)(2,1)} %get-tuple-element.168), channel_id=1, source_target_pairs={{0,12},{4,0},{8,4},{12,8},{1,13},{5,1},{9,5},{13,9},{2,14},{6,2},{... | collective-permute-start | bytes 516104 | tf_op jit(solution)/shard_map/ppermute | solution.py:33
  335.0 34.7 %collective-permute-start.17 = (bf16[7,48,256]{2,1,0:T(8,128)(2,1)}, bf16[7,48,256]{2,1,0:T(8,128)(2,1)S(1)}, u32[]{:S(2)}, u32[]{:S(2)}) collective-permute-start(bf16[7,48,256]{2,1,0:T(8,128)(2,1)} %get-tuple-element.163), channel_id=1, source_target_pairs={{0,8},{4,12},{8,0},{12,4},{1,9},{5,13},{9,1},{13,5},{2,10},{6,14},... | collective-permute-start | bytes 516104 | tf_op jit(solution)/shard_map/ppermute | solution.py:33
  406.5 32.3 %collective-permute-start.30 = (bf16[7,96,256]{2,1,0:T(8,128)(2,1)}, bf16[7,96,256]{2,1,0:T(8,128)(2,1)S(1)}, u32[]{:S(2)}, u32[]{:S(2)}) collective-permute-start(bf16[7,96,256]{2,1,0:T(8,128)(2,1)} %get-tuple-element.179), channel_id=1, source_target_pairs={{0,1},{1,2},{2,3},{3,0},{4,5},{5,6},{6,7},{7,4},{8,9},{9,10},{10,1... | collective-permute-start | bytes 1032200 | tf_op jit(solution)/shard_map/ppermute | solution.py:33
  406.5 32.3 %collective-permute-start.31 = (bf16[7,96,256]{2,1,0:T(8,128)(2,1)}, bf16[7,96,256]{2,1,0:T(8,128)(2,1)S(1)}, u32[]{:S(2)}, u32[]{:S(2)}) collective-permute-start(bf16[7,96,256]{2,1,0:T(8,128)(2,1)} %get-tuple-element.180), channel_id=1, source_target_pairs={{0,2},{1,3},{2,0},{3,1},{4,6},{5,7},{6,4},{7,5},{8,10},{9,11},{10,... | collective-permute-start | bytes 1032200 | tf_op jit(solution)/shard_map/ppermute | solution.py:33
  408.3 31.7 %collective-permute-start.32 = (bf16[7,96,256]{2,1,0:T(8,128)(2,1)}, bf16[7,96,256]{2,1,0:T(8,128)(2,1)S(1)}, u32[]{:S(2)}, u32[]{:S(2)}) collective-permute-start(bf16[7,96,256]{2,1,0:T(8,128)(2,1)} %get-tuple-element.181), channel_id=1, source_target_pairs={{0,3},{1,0},{2,1},{3,2},{4,7},{5,4},{6,5},{7,6},{8,11},{9,8},{10,9... | collective-permute-start | bytes 1032200 | tf_op jit(solution)/shard_map/ppermute | solution.py:33
  426.1 35.6 %collective-permute-start.41 = (bf16[7,48,256]{2,1,0:T(8,128)(2,1)S(1)}, bf16[7,48,256]{2,1,0:T(8,128)(2,1)S(1)}, u32[]{:S(2)}, u32[]{:S(2)}) collective-permute-start(bf16[7,48,256]{2,1,0:T(8,128)(2,1)S(1)} %copy-done.65), channel_id=1, source_target_pairs={{0,8},{4,12},{8,0},{12,4},{1,9},{5,13},{9,1},{13,5},{2,10},{6,14},... | collective-permute-start | bytes 516104 | tf_op jit(solution)/shard_map/ppermute | solution.py:33
  435.2 30.1 %collective-permute-start.42 = (bf16[7,48,256]{2,1,0:T(8,128)(2,1)S(1)}, bf16[7,48,256]{2,1,0:T(8,128)(2,1)S(1)}, u32[]{:S(2)}, u32[]{:S(2)}) collective-permute-start(bf16[7,48,256]{2,1,0:T(8,128)(2,1)S(1)} %copy-done.64), channel_id=1, source_target_pairs={{0,12},{4,0},{8,4},{12,8},{1,13},{5,1},{9,5},{13,9},{2,14},{6,2},{... | collective-permute-start | bytes 516104 | tf_op jit(solution)/shard_map/ppermute | solution.py:33
  438.8 30.9 %collective-permute-start.37 = (bf16[7,96,256]{2,1,0:T(8,128)(2,1)}, bf16[7,96,256]{2,1,0:T(8,128)(2,1)S(1)}, u32[]{:S(2)}, u32[]{:S(2)}) collective-permute-start(bf16[7,96,256]{2,1,0:T(8,128)(2,1)} %get-tuple-element.188), channel_id=1, source_target_pairs={{0,1},{1,2},{2,3},{3,0},{4,5},{5,6},{6,7},{7,4},{8,9},{9,10},{10,1... | collective-permute-start | bytes 1032200 | tf_op jit(solution)/shard_map/ppermute | solution.py:33
  438.8 30.9 %collective-permute-start.38 = (bf16[7,96,256]{2,1,0:T(8,128)(2,1)}, bf16[7,96,256]{2,1,0:T(8,128)(2,1)S(1)}, u32[]{:S(2)}, u32[]{:S(2)}) collective-permute-start(bf16[7,96,256]{2,1,0:T(8,128)(2,1)} %get-tuple-element.189), channel_id=1, source_target_pairs={{0,2},{1,3},{2,0},{3,1},{4,6},{5,7},{6,4},{7,5},{8,10},{9,11},{10,... | collective-permute-start | bytes 1032200 | tf_op jit(solution)/shard_map/ppermute | solution.py:33
  440.1 30.7 %collective-permute-start.39 = (bf16[7,96,256]{2,1,0:T(8,128)(2,1)}, bf16[7,96,256]{2,1,0:T(8,128)(2,1)S(1)}, u32[]{:S(2)}, u32[]{:S(2)}) collective-permute-start(bf16[7,96,256]{2,1,0:T(8,128)(2,1)} %get-tuple-element.190), channel_id=1, source_target_pairs={{0,3},{1,0},{2,1},{3,2},{4,7},{5,4},{6,5},{7,6},{8,11},{9,8},{10,9... | collective-permute-start | bytes 1032200 | tf_op jit(solution)/shard_map/ppermute | solution.py:33
  461.8 54.1 %collective-permute-start.36 = (bf16[7,90,1024]{2,1,0:T(8,128)(2,1)}, bf16[7,90,1024]{2,1,0:T(8,128)(2,1)S(1)}, u32[]{:S(2)}, u32[]{:S(2)}) collective-permute-start(bf16[7,90,1024]{2,1,0:T(8,128)(2,1)} %get-tuple-element.187), channel_id=1, source_target_pairs={{0,16},{1,17},{2,18},{3,19},{4,20},{5,21},{6,22},{7,23},{8,24},{9,... | collective-permute-start | bytes 3870728 | tf_op jit(solution)/shard_map/ppermute | solution.py:491
  491.8 40.7 %collective-permute-start.52 = (bf16[7,90,1024]{2,1,0:T(8,128)(2,1)}, bf16[7,90,1024]{2,1,0:T(8,128)(2,1)S(1)}, u32[]{:S(2)}, u32[]{:S(2)}) collective-permute-start(bf16[7,90,1024]{2,1,0:T(8,128)(2,1)} %get-tuple-element.210), channel_id=1, source_target_pairs={{0,16},{1,17},{2,18},{3,19},{4,20},{5,21},{6,22},{7,23},{8,24},{9,... | collective-permute-start | bytes 3870728 | tf_op jit(solution)/shard_map/ppermute | solution.py:491
  526.1 32.9 %collective-permute-start.50 = (bf16[7,96,256]{2,1,0:T(8,128)(2,1)}, bf16[7,96,256]{2,1,0:T(8,128)(2,1)S(1)}, u32[]{:S(2)}, u32[]{:S(2)}) collective-permute-start(bf16[7,96,256]{2,1,0:T(8,128)(2,1)} %get-tuple-element.208), channel_id=1, source_target_pairs={{0,2},{1,3},{2,0},{3,1},{4,6},{5,7},{6,4},{7,5},{8,10},{9,11},{10,... | collective-permute-start | bytes 1032200 | tf_op jit(solution)/shard_map/ppermute | solution.py:33
  527.3 33.1 %collective-permute-start.51 = (bf16[7,96,256]{2,1,0:T(8,128)(2,1)}, bf16[7,96,256]{2,1,0:T(8,128)(2,1)S(1)}, u32[]{:S(2)}, u32[]{:S(2)}) collective-permute-start(bf16[7,96,256]{2,1,0:T(8,128)(2,1)} %get-tuple-element.209), channel_id=1, source_target_pairs={{0,3},{1,0},{2,1},{3,2},{4,7},{5,4},{6,5},{7,6},{8,11},{9,8},{10,9... | collective-permute-start | bytes 1032200 | tf_op jit(solution)/shard_map/ppermute | solution.py:33
  530.6 34.3 %collective-permute-start.43 = (bf16[7,96,256]{2,1,0:T(8,128)(2,1)}, bf16[7,96,256]{2,1,0:T(8,128)(2,1)S(1)}, u32[]{:S(2)}, u32[]{:S(2)}) collective-permute-start(bf16[7,96,256]{2,1,0:T(8,128)(2,1)} %get-tuple-element.200), channel_id=1, source_target_pairs={{0,1},{1,2},{2,3},{3,0},{4,5},{5,6},{6,7},{7,4},{8,9},{9,10},{10,1... | collective-permute-start | bytes 1032200 | tf_op jit(solution)/shard_map/ppermute | solution.py:33
  532.5 32.4 %collective-permute-start.44 = (bf16[7,96,256]{2,1,0:T(8,128)(2,1)}, bf16[7,96,256]{2,1,0:T(8,128)(2,1)S(1)}, u32[]{:S(2)}, u32[]{:S(2)}) collective-permute-start(bf16[7,96,256]{2,1,0:T(8,128)(2,1)} %get-tuple-element.201), channel_id=1, source_target_pairs={{0,2},{1,3},{2,0},{3,1},{4,6},{5,7},{6,4},{7,5},{8,10},{9,11},{10,... | collective-permute-start | bytes 1032200 | tf_op jit(solution)/shard_map/ppermute | solution.py:33
  533.2 31.7 %collective-permute-start.45 = (bf16[7,96,256]{2,1,0:T(8,128)(2,1)}, bf16[7,96,256]{2,1,0:T(8,128)(2,1)S(1)}, u32[]{:S(2)}, u32[]{:S(2)}) collective-permute-start(bf16[7,96,256]{2,1,0:T(8,128)(2,1)} %get-tuple-element.202), channel_id=1, source_target_pairs={{0,3},{1,0},{2,1},{3,2},{4,7},{5,4},{6,5},{7,6},{8,11},{9,8},{10,9... | collective-permute-start | bytes 1032200 | tf_op jit(solution)/shard_map/ppermute | solution.py:33
  559.1 31.9 %collective-permute-start.53 = (bf16[7,90,1024]{2,1,0:T(8,128)(2,1)S(1)}, bf16[7,90,1024]{2,1,0:T(8,128)(2,1)S(1)}, u32[]{:S(2)}, u32[]{:S(2)}) collective-permute-start(bf16[7,90,1024]{2,1,0:T(8,128)(2,1)S(1)} %copy-done.26), channel_id=1, source_target_pairs={{0,16},{1,17},{2,18},{3,19},{4,20},{5,21},{6,22},{7,23},{8,24},{9,... | collective-permute-start | bytes 3870728 | tf_op jit(solution)/shard_map/ppermute | solution.py:491
  586.0 33.6 %collective-permute-start.54 = (bf16[7,90,1024]{2,1,0:T(8,128)(2,1)}, bf16[7,90,1024]{2,1,0:T(8,128)(2,1)S(1)}, u32[]{:S(2)}, u32[]{:S(2)}) collective-permute-start(bf16[7,90,1024]{2,1,0:T(8,128)(2,1)} %get-tuple-element.215), channel_id=1, source_target_pairs={{0,16},{1,17},{2,18},{3,19},{4,20},{5,21},{6,22},{7,23},{8,24},{9,... | collective-permute-start | bytes 3870728 | tf_op jit(solution)/shard_map/ppermute | solution.py:491
  596.9 30.1 %collective-permute-start.58 = (bf16[7,96,256]{2,1,0:T(8,128)(2,1)}, bf16[7,96,256]{2,1,0:T(8,128)(2,1)S(1)}, u32[]{:S(2)}, u32[]{:S(2)}) collective-permute-start(bf16[7,96,256]{2,1,0:T(8,128)(2,1)} %get-tuple-element.221), channel_id=1, source_target_pairs={{0,1},{1,2},{2,3},{3,0},{4,5},{5,6},{6,7},{7,4},{8,9},{9,10},{10,1... | collective-permute-start | bytes 1032200 | tf_op jit(solution)/shard_map/ppermute | solution.py:33
  597.1 31.3 %collective-permute-start.59 = (bf16[7,96,256]{2,1,0:T(8,128)(2,1)}, bf16[7,96,256]{2,1,0:T(8,128)(2,1)S(1)}, u32[]{:S(2)}, u32[]{:S(2)}) collective-permute-start(bf16[7,96,256]{2,1,0:T(8,128)(2,1)} %get-tuple-element.222), channel_id=1, source_target_pairs={{0,2},{1,3},{2,0},{3,1},{4,6},{5,7},{6,4},{7,5},{8,10},{9,11},{10,... | collective-permute-start | bytes 1032200 | tf_op jit(solution)/shard_map/ppermute | solution.py:33
  598.5 35.8 %collective-permute-start.60 = (bf16[7,96,256]{2,1,0:T(8,128)(2,1)}, bf16[7,96,256]{2,1,0:T(8,128)(2,1)S(1)}, u32[]{:S(2)}, u32[]{:S(2)}) collective-permute-start(bf16[7,96,256]{2,1,0:T(8,128)(2,1)} %get-tuple-element.223), channel_id=1, source_target_pairs={{0,3},{1,0},{2,1},{3,2},{4,7},{5,4},{6,5},{7,6},{8,11},{9,8},{10,9... | collective-permute-start | bytes 1032200 | tf_op jit(solution)/shard_map/ppermute | solution.py:33
  625.6 27.5 %collective-permute-start.62 = (bf16[7,96,256]{2,1,0:T(8,128)(2,1)}, bf16[7,96,256]{2,1,0:T(8,128)(2,1)S(1)}, u32[]{:S(2)}, u32[]{:S(2)}) collective-permute-start(bf16[7,96,256]{2,1,0:T(8,128)(2,1)} %get-tuple-element.227), channel_id=1, source_target_pairs={{0,2},{1,3},{2,0},{3,1},{4,6},{5,7},{6,4},{7,5},{8,10},{9,11},{10,... | collective-permute-start | bytes 1032200 | tf_op jit(solution)/shard_map/ppermute | solution.py:33
  706.5 31.3 %collective-permute-start.80 = (bf16[7,48,256]{2,1,0:T(8,128)(2,1)}, bf16[7,48,256]{2,1,0:T(8,128)(2,1)S(1)}, u32[]{:S(2)}, u32[]{:S(2)}) collective-permute-start(bf16[7,48,256]{2,1,0:T(8,128)(2,1)} %get-tuple-element.248), channel_id=1, source_target_pairs={{0,8},{4,12},{8,0},{12,4},{1,9},{5,13},{9,1},{13,5},{2,10},{6,14},... | collective-permute-start | bytes 516104 | tf_op jit(solution)/shard_map/ppermute | solution.py:33
  709.2 28.6 %collective-permute-start.81 = (bf16[7,48,256]{2,1,0:T(8,128)(2,1)}, bf16[7,48,256]{2,1,0:T(8,128)(2,1)S(1)}, u32[]{:S(2)}, u32[]{:S(2)}) collective-permute-start(bf16[7,48,256]{2,1,0:T(8,128)(2,1)} %get-tuple-element.249), channel_id=1, source_target_pairs={{0,12},{4,0},{8,4},{12,8},{1,13},{5,1},{9,5},{13,9},{2,14},{6,2},{... | collective-permute-start | bytes 516104 | tf_op jit(solution)/shard_map/ppermute | solution.py:33
  720.1 28.1 %collective-permute-start.77 = (bf16[7,48,256]{2,1,0:T(8,128)(2,1)}, bf16[7,48,256]{2,1,0:T(8,128)(2,1)S(1)}, u32[]{:S(2)}, u32[]{:S(2)}) collective-permute-start(bf16[7,48,256]{2,1,0:T(8,128)(2,1)} %get-tuple-element.244), channel_id=1, source_target_pairs={{0,8},{4,12},{8,0},{12,4},{1,9},{5,13},{9,1},{13,5},{2,10},{6,14},... | collective-permute-start | bytes 516104 | tf_op jit(solution)/shard_map/ppermute | solution.py:33
  742.4 27.5 %collective-permute-start.98 = (bf16[7,96,256]{2,1,0:T(8,128)(2,1)}, bf16[7,96,256]{2,1,0:T(8,128)(2,1)S(1)}, u32[]{:S(2)}, u32[]{:S(2)}) collective-permute-start(bf16[7,96,256]{2,1,0:T(8,128)(2,1)} %get-tuple-element.272), channel_id=1, source_target_pairs={{0,2},{1,3},{2,0},{3,1},{4,6},{5,7},{6,4},{7,5},{8,10},{9,11},{10,... | collective-permute-start | bytes 1032200 | tf_op jit(solution)/shard_map/ppermute | solution.py:33
  769.9 55.5 %collective-permute-start.92 = (bf16[7,96,256]{2,1,0:T(8,128)(2,1)}, bf16[7,96,256]{2,1,0:T(8,128)(2,1)S(1)}, u32[]{:S(2)}, u32[]{:S(2)}) collective-permute-start(bf16[7,96,256]{2,1,0:T(8,128)(2,1)} %get-tuple-element.266), channel_id=1, source_target_pairs={{0,2},{1,3},{2,0},{3,1},{4,6},{5,7},{6,4},{7,5},{8,10},{9,11},{10,... | collective-permute-start | bytes 1032200 | tf_op jit(solution)/shard_map/ppermute | solution.py:33
  773.6 51.9 %collective-permute-start.93 = (bf16[7,96,256]{2,1,0:T(8,128)(2,1)}, bf16[7,96,256]{2,1,0:T(8,128)(2,1)S(1)}, u32[]{:S(2)}, u32[]{:S(2)}) collective-permute-start(bf16[7,96,256]{2,1,0:T(8,128)(2,1)} %get-tuple-element.267), channel_id=1, source_target_pairs={{0,3},{1,0},{2,1},{3,2},{4,7},{5,4},{6,5},{7,6},{8,11},{9,8},{10,9... | collective-permute-start | bytes 1032200 | tf_op jit(solution)/shard_map/ppermute | solution.py:33
  774.9 50.6 %collective-permute-start.85 = (bf16[7,96,256]{2,1,0:T(8,128)(2,1)}, bf16[7,96,256]{2,1,0:T(8,128)(2,1)S(1)}, u32[]{:S(2)}, u32[]{:S(2)}) collective-permute-start(bf16[7,96,256]{2,1,0:T(8,128)(2,1)} %get-tuple-element.257), channel_id=1, source_target_pairs={{0,1},{1,2},{2,3},{3,0},{4,5},{5,6},{6,7},{7,4},{8,9},{9,10},{10,1... | collective-permute-start | bytes 1032200 | tf_op jit(solution)/shard_map/ppermute | solution.py:33
  780.8 44.7 %collective-permute-start.86 = (bf16[7,96,256]{2,1,0:T(8,128)(2,1)}, bf16[7,96,256]{2,1,0:T(8,128)(2,1)}, u32[]{:S(2)}, u32[]{:S(2)}) collective-permute-start(bf16[7,96,256]{2,1,0:T(8,128)(2,1)} %get-tuple-element.258), channel_id=1, source_target_pairs={{0,2},{1,3},{2,0},{3,1},{4,6},{5,7},{6,4},{7,5},{8,10},{9,11},{10,... | collective-permute-start | bytes 1032200 | tf_op jit(solution)/shard_map/ppermute | solution.py:33
  788.3 37.2 %collective-permute-start.87 = (bf16[7,96,256]{2,1,0:T(8,128)(2,1)}, bf16[7,96,256]{2,1,0:T(8,128)(2,1)}, u32[]{:S(2)}, u32[]{:S(2)}) collective-permute-start(bf16[7,96,256]{2,1,0:T(8,128)(2,1)} %get-tuple-element.259), channel_id=1, source_target_pairs={{0,3},{1,0},{2,1},{3,2},{4,7},{5,4},{6,5},{7,6},{8,11},{9,8},{10,9... | collective-permute-start | bytes 1032200 | tf_op jit(solution)/shard_map/ppermute | solution.py:33
  (179 other events, 3089.5 us)
Sparse Core Ops, SparseCore 0:
  15.4 83.4 all-gather.8
  101.0 79.2 all-gather.12
  181.8 163.3 all-gather.10
  346.7 134.4 all-gather.14
